TPU v7x, 32 devices: a whole 2x2x4 slice. The times are simulated.
32 devices in a mesh: dp: 8 (over z, core), tp: 4 (over y, x).
Axes of the slice: x: 2, y: 2, z: 4, core: 2. Of those that a mesh axis runs over, the one named last changes fastest.
Arguments:
- tokens: bfloat16 [4096, 4096], P('dp'), may hold values from -6 to 6
- gain: float32 [4096], replicated, may hold values from 0.1 to 1.9
- router: float32 [4096, 8], replicated, may hold values from -0.09375 to 0.09375
- routes: int32 [4096, 2], P('dp'), may hold values from 0 to 7, all different within a row
- w_gate: bfloat16 [2, 4096, 1024], P(None, 'dp', 'tp'), may hold values from -0.125 to 0.125
- w_up: bfloat16 [2, 4096, 1024], P(None, 'dp', 'tp'), may hold values from -0.125 to 0.125
- w_down: bfloat16 [2, 1024, 4096], P(None, 'dp', 'tp'), may hold values from -0.25 to 0.25
Outputs:
- mixed: bfloat16 [4096, 4096], P('dp', 'tp')
Inputs may be any that keep to these rules, and one draw needn't show every extreme that they name: `routes`: each row names two different experts.
All inputs are finite; a program needn't handle non-finite values.
Results may differ from a plain program's by a relative error of at most 0.0065.
Values may be sent and summed in bfloat16 or wider, within the bound.
A program may use at most 64 MiB of HBM per device.

v0:
```python
import jax
import jax.numpy as jnp
from jax import lax
from jax.sharding import PartitionSpec as P

EPS = 1e-06
ROUTE_SCALE = 2.5


def per_device(tokens, gain, router, routes, w_gate, w_up, w_down):
    values = tokens.astype(jnp.float32)
    square = jnp.mean(values * values, axis=-1, keepdims=True)
    normed = (values * lax.rsqrt(square + EPS) * gain).astype(jnp.bfloat16)
    scores = jax.nn.sigmoid(
        jnp.dot(normed.astype(jnp.float32), router, precision=lax.Precision.HIGHEST)
    )
    labels = jnp.arange(router.shape[1], dtype=jnp.int32)
    picked_mask = (routes[:, :, None] == labels[None, None, :]).astype(jnp.float32)
    picked = jnp.sum(picked_mask * scores[:, None, :], axis=-1)
    chosen = jnp.sum(picked_mask, axis=1)
    combine = chosen * scores * ROUTE_SCALE / jnp.sum(picked, axis=-1, keepdims=True)
    held_weights = combine[:, : w_gate.shape[0]]
    full_gate, full_up, full_down = (
        lax.all_gather(w_gate, "dp", axis=1, tiled=True),
        lax.all_gather(w_up, "dp", axis=1, tiled=True),
        lax.all_gather(w_down, "dp", axis=1, tiled=True),
    )
    gate_value = jnp.einsum("td,edf->tef", normed, full_gate, preferred_element_type=jnp.float32)
    up_value = jnp.einsum("td,edf->tef", normed, full_up, preferred_element_type=jnp.float32)
    hidden = (jax.nn.silu(gate_value) * up_value * held_weights[:, :, None]).astype(jnp.bfloat16)
    whole_hidden = lax.all_gather(hidden, "tp", axis=2, tiled=True)
    mixed = jnp.einsum("tef,efd->td", whole_hidden, full_down, preferred_element_type=jnp.float32)
    return mixed.astype(jnp.bfloat16)


def solution(mesh):
    return jax.shard_map(
        per_device,
        mesh=mesh,
        in_specs=(
            P("dp", None),
            P(),
            P(),
            P("dp", None),
            P(None, "dp", "tp"),
            P(None, "dp", "tp"),
            P(None, "dp", "tp"),
        ),
        out_specs=P("dp", "tp"),
        check_vma=False,
    )
```

profile of v0, /device:TPU:0, one launch (start us, length us, event | category | flops | bytes accessed | tf_op | source)
XLA Modules:
  0.0 201.4 jit_solution(2412415738272658088)
XLA Ops:
  6.5 0.0 copy-start
  6.5 0.0 copy-start.3
  6.5 0.0 all-gather.5.cloned.1.call-start
  6.5 0.7 all-gather.5.cloned.1.call-update
  7.3 0.0 all-gather.7.cloned.1.call-start
  7.3 0.7 all-gather.7.cloned.1.call-update
  8.0 0.0 all-gather.11.cloned.1.call-start
  8.1 0.7 all-gather.11.cloned.1.call-update
  8.7 0.0 all-gather.9.cloned.1.call-start
  8.8 0.0 copy-start.1
  8.8 3.2 %fusion = f32[512]{0:T(512)S(1)} fusion(bf16[512,4096]{1,0:T(8,128)(2,1)} %param.7), kind=kLoop, calls=%fused_computation.2 | loop fusion | flops 6290944 | bytes 4196352 | tf_op jit(solution)/shard_map/reduce_sum | solution.py:12
  12.1 0.0 copy-done
  12.1 0.0 copy-done.3
  12.1 0.2 copy-done.1
  12.2 3.4 %fusion.18 = f32[512,8]{0,1:T(8,128)S(1)} fusion(f32[4096,8]{0,1:T(8,128)S(1)} %copy-done, bf16[512,4096]{1,0:T(8,128)(2,1)S(1)} %copy-done.1, f32[4096]{0:T(1024)S(1)} %copy-done.3, f32[512]{0:T(512)S(1)} %add_rsqrt_fusion), kind=kOutput, calls=%fused_computation.16 | convolution fusion | flops 209727488 | bytes 4360192 | tf_op jit(solution)/shard_map/dot_general | solution.py:15
  15.7 0.0 copy-done.2
  15.7 42.8 %all-gather.5.cloned.1.call-done = bf16[2,4096,256]{2,1,0:T(8,128)(2,1)} async-done(((bf16[2,512,256]{2,1,0:T(8,128)(2,1)}), bf16[2,4096,256]{2,1,0:T(8,128)(2,1)}) %all-gather.5.cloned.1.call-update) | async-done | bytes 4194320 | tf_op jit(solution)/shard_map/all_gather | solution.py:24
  58.6 5.8 %fusion.5 = f32[512,2,256]{2,0,1:T(8,128)S(1)} fusion(bf16[2,4096,256]{2,1,0:T(8,128)(2,1)} %all-gather.5.cloned.1.call-done, bf16[512,4096]{1,0:T(8,128)(2,1)} %param.7, f32[4096]{0:T(1024)S(1)} %copy-done.3, f32[512]{0:T(512)S(1)} %add_rsqrt_fusion), kind=kOutput, calls=%fused_computation.7 | convolution fusion | flops 2155872256 | bytes 9455616 | tf_op jit(solution)/shard_map/td,edf->tef/dot_general | solution.py:28
  64.4 41.5 %all-gather.7.cloned.1.call-done = bf16[2,4096,256]{2,1,0:T(8,128)(2,1)} async-done(((bf16[2,512,256]{2,1,0:T(8,128)(2,1)}), bf16[2,4096,256]{2,1,0:T(8,128)(2,1)}) %all-gather.7.cloned.1.call-update) | async-done | bytes 4194320 | tf_op jit(solution)/shard_map/all_gather | solution.py:25
  105.9 6.8 %fusion.13 = bf16[512,2,256]{2,0,1:T(8,128)(2,1)} fusion(bf16[2,4096,256]{2,1,0:T(8,128)(2,1)} %all-gather.7.cloned.1.call-done, f32[512,2,256]{2,0,1:T(8,128)S(1)} %fusion.5, f32[512,2]{0,1:T(2,128)S(1)} %fusion.20, bf16[512,4096]{1,0:T(8,128)(2,1)} %param.7, f32[4096]{0:T(1024)S(1)} %copy-done.3, f32[512]{0:T(512)S(1)} %add_rsqrt_fusion), kind=kOutput, calls=%fused_computation.12 | convolution fusion | flops 2157707264 | bytes 9984000 | tf_op jit(solution)/shard_map/td,edf->tef/dot_general | solution.py:29
  112.6 0.0 all-gather.9.cloned.1.call-update
  112.7 40.5 %all-gather.11.cloned.1.call-done = bf16[2,1024,1024]{2,1,0:T(8,128)(2,1)} async-done(((bf16[2,128,1024]{2,1,0:T(8,128)(2,1)}), bf16[2,1024,1024]{2,1,0:T(8,128)(2,1)}) %all-gather.11.cloned.1.call-update) | async-done | bytes 4194320 | tf_op jit(solution)/shard_map/all_gather | solution.py:26
  153.2 35.6 %all-gather.9.cloned.1.call-done = bf16[512,2,1024]{2,0,1:T(8,128)(2,1)} async-done(((bf16[512,2,256]{2,0,1:T(8,128)(2,1)}), bf16[512,2,1024]{2,0,1:T(8,128)(2,1)}) %all-gather.9.cloned.1.call-update) | async-done | bytes 2097168 | tf_op jit(solution)/shard_map/all_gather | solution.py:31
  188.8 6.1 %bitcast_convert_fusion = bf16[512,1024]{1,0:T(8,128)(2,1)} fusion(bf16[512,2,1024]{2,0,1:T(8,128)(2,1)} %all-gather.9.cloned.1.call-done, bf16[2,1024,1024]{2,1,0:T(8,128)(2,1)} %all-gather.11.cloned.1.call-done), kind=kOutput, calls=%fused_computation.9 | convolution fusion | flops 2148007936 | bytes 7340032 | tf_op jit(solution)/shard_map/tef,efd->td/dot_general | solution.py:32
  (4 shorter events, 0.0 us)
Async XLA Ops:
  6.5 5.5 %copy-start = (f32[4096,8]{0,1:T(8,128)S(1)}, f32[4096,8]{0,1:T(8,128)}, u32[]{:S(2)}) copy-start(f32[4096,8]{0,1:T(8,128)} %param.9) | copy-start | bytes 393220
  6.5 5.5 %copy-start.3 = (f32[4096]{0:T(1024)S(1)}, f32[4096]{0:T(1024)}, u32[]{:S(2)}) copy-start(f32[4096]{0:T(1024)} %param.8) | copy-start | bytes 49156
  6.5 52.0 %all-gather.5.cloned.1.call-start = ((), (), s32[]{:S(2)}) async-start(), calls=%async_computation | async-start | bytes 4718592 | tf_op jit(solution)/shard_map/all_gather | solution.py:24
  7.3 98.6 %all-gather.7.cloned.1.call-start = ((), (), s32[]{:S(2)}) async-start(), calls=%async_computation.1 | async-start | bytes 4718592 | tf_op jit(solution)/shard_map/all_gather | solution.py:25
  8.0 145.2 %all-gather.11.cloned.1.call-start = ((), (), s32[]{:S(2)}) async-start(), calls=%async_computation.3 | async-start | bytes 4718592 | tf_op jit(solution)/shard_map/all_gather | solution.py:26
  8.7 180.0 %all-gather.9.cloned.1.call-start = ((), (), s32[]{:S(2)}) async-start(), calls=%async_computation.2 | async-start | bytes 2621440 | tf_op jit(solution)/shard_map/all_gather | solution.py:31
  8.8 3.5 %copy-start.1 = (bf16[512,4096]{1,0:T(8,128)(2,1)S(1)}, bf16[512,4096]{1,0:T(8,128)(2,1)}, u32[]{:S(2)}) copy-start(bf16[512,4096]{1,0:T(8,128)(2,1)} %param.7) | copy-start | bytes 12582916
  12.0 3.6 %copy-start.2 = (s32[512,2]{0,1:T(2,128)S(1)}, s32[512,2]{0,1:T(2,128)}, u32[]{:S(2)}) copy-start(s32[512,2]{0,1:T(2,128)} %param.10) | copy-start | bytes 12292
Sparse Core Ops, SparseCore 0:
  8.9 49.5 all-gather.4
  60.2 45.6 all-gather.6
  107.5 45.6 all-gather.10
  154.9 33.8 all-gather.8
where the time goes:
time: 202 us; the launch traced here: 201 us
  waiting for transfers between devices  162 us (80%)
  matrix products  22.2 us (11%)
  between operations  13.2 us (7%)
  other arithmetic  3.27 us (2%)
    all_gather x1, waiting for transfers between devices, per_device(): lax.all_gather(w_gate, 'dp', axis=1, tiled=True)  42.8 us
    all_gather x1, waiting for transfers between devices, per_device(): lax.all_gather(w_up, 'dp', axis=1, tiled=True)  41.5 us
    all_gather x1, waiting for transfers between devices, per_device(): lax.all_gather(w_down, 'dp', axis=1, tiled=True)  40.5 us
    all_gather x1, waiting for transfers between devices, per_device(): whole_hidden = lax.all_gather(hidden, 'tp', axis=2, tiled=True)  35.6 us
    dot_general x1, matrix products, per_device(): jnp.einsum('td,edf->tef', normed, full_up, preferred_element_type=jnp.flo...  6.76 us
    dot_general x1, matrix products, per_device(): jnp.einsum('tef,efd->td', whole_hidden, full_down, preferred_element_type...  6.12 us
    dot_general x1, matrix products, per_device(): jnp.einsum('td,edf->tef', normed, full_gate, preferred_element_type=jnp.f...  5.84 us
  transfers between devices with their start and end apart: 4, of which 4 were waited for; matrix products, arithmetic and copies ran while one was open for 10% of the time, Pallas kernels for 0%

commit v1 on v0

--- a/solution.py
+++ b/solution.py
@@ -5,6 +5,17 @@
 
 EPS = 1e-06
 ROUTE_SCALE = 2.5
+
+
+def pass_along(array, name, d):
+    count = lax.axis_size(name)
+    right = [(i, (i + 1) % count) for i in range(count)]
+    parts = [array]
+    for reach in range(1, count):
+        parts = [lax.ppermute(parts[0], name, right), *parts]
+    result = jnp.concatenate(parts, axis=d)
+    shift = (lax.axis_index(name) + 1) * parts[-1].shape[d]
+    return jnp.roll(result, shift, axis=d)
 
 
 def per_device(tokens, gain, router, routes, w_gate, w_up, w_down):
@@ -28,7 +39,7 @@
     gate_value = jnp.einsum("td,edf->tef", normed, full_gate, preferred_element_type=jnp.float32)
     up_value = jnp.einsum("td,edf->tef", normed, full_up, preferred_element_type=jnp.float32)
     hidden = (jax.nn.silu(gate_value) * up_value * held_weights[:, :, None]).astype(jnp.bfloat16)
-    whole_hidden = lax.all_gather(hidden, "tp", axis=2, tiled=True)
+    whole_hidden = pass_along(hidden, "tp", 2)
     mixed = jnp.einsum("tef,efd->td", whole_hidden, full_down, preferred_element_type=jnp.float32)
     return mixed.astype(jnp.bfloat16)
 

time: 202 us -> 174 us (0.86)
  waiting for transfers between devices: 162 us -> 123 us
  local copies, waits for them, and re-layouts: 0.18 us -> 11 us
  starting transfers between devices: 0.12 us -> 2.17 us
    ppermute x0 -> x3, waiting for transfers between devices: none -> 40.6 us  [pass_along(): parts = [lax.ppermute(parts[0], name, right), *parts]]
    all_gather x1, waiting for transfers between devices: 40.5 us -> 0.01 us  [per_device(): lax.all_gather(w_down, 'dp', axis=1, tiled=True)]
    all_gather x1 -> x0, waiting for transfers between devices: 35.6 us -> none  [per_device(): whole_hidden = lax.all_gather(hidden, 'tp', axis=2, tiled=True)]
    unnamed x8 -> x17, local copies, waits for them, and re-layouts: 0.18 us -> 10.2 us
    all_gather x1, waiting for transfers between devices: 42.8 us -> 40.1 us  [per_device(): lax.all_gather(w_gate, 'dp', axis=1, tiled=True)]
    ppermute x0 -> x3, starting transfers between devices: none -> 2.09 us  [pass_along(): parts = [lax.ppermute(parts[0], name, right), *parts]]
  transfers between devices with their start and end apart: 4 -> 6, of which waited for: 4 -> 5; matrix products, arithmetic and copies ran while one was open for 10% -> 16% of each run, Pallas kernels for 0% -> 0%
where the time goes in v1:
time: 174 us
  waiting for transfers between devices  123 us (71%)
  matrix products  21.5 us (12%)
  between operations  13.2 us (8%)
  local copies, waits for them, and re-layouts  11 us (6%)
  other arithmetic  3.27 us (2%)
  starting transfers between devices  2.17 us (1%)
    all_gather x1, waiting for transfers between devices, per_device(): lax.all_gather(w_up, 'dp', axis=1, tiled=True)  41.4 us
    ppermute x3, waiting for transfers between devices, pass_along(): parts = [lax.ppermute(parts[0], name, right), *parts]  40.6 us
    all_gather x1, waiting for transfers between devices, per_device(): lax.all_gather(w_gate, 'dp', axis=1, tiled=True)  40.1 us
    unnamed x17, local copies, waits for them, and re-layouts  10.2 us
    dot_general x1, matrix products, per_device(): jnp.einsum('tef,efd->td', whole_hidden, full_down, preferred_element_type...  6.14 us
    dot_general x1, matrix products, per_device(): jnp.einsum('td,edf->tef', normed, full_up, preferred_element_type=jnp.flo...  6.04 us
    dot_general x1, matrix products, per_device(): jnp.einsum('td,edf->tef', normed, full_gate, preferred_element_type=jnp.f...  5.91 us
  transfers between devices with their start and end apart: 6, of which 5 were waited for; matrix products, arithmetic and copies ran while one was open for 16% of the time, Pallas kernels for 0%

profile of v1, /device:TPU:0, one launch (start us, length us, event | category | flops | bytes accessed | tf_op | source)
XLA Modules:
  0.0 174.0 jit_solution(8103222563868947899)
XLA Ops:
  6.5 2.1 %copy.13 = bf16[2,512,256]{1,2,0:T(8,128)(2,1)} copy(bf16[2,512,256]{2,1,0:T(8,128)(2,1)} %param.11) | data formatting | bytes 1048576 | tf_op args[4]
  8.7 2.0 %copy.14 = bf16[2,512,256]{1,2,0:T(8,128)(2,1)} copy(bf16[2,512,256]{2,1,0:T(8,128)(2,1)} %param.12) | data formatting | bytes 1048576 | tf_op args[5]
  10.8 0.7 all-gather.8.cloned.1.call-update
  11.5 3.2 %fusion = f32[512]{0:T(512)S(1)} fusion(bf16[512,4096]{1,0:T(8,128)(2,1)} %param.7), kind=kLoop, calls=%fused_computation.2 | loop fusion | flops 6290944 | bytes 4196352 | tf_op jit(solution)/shard_map/reduce_sum | solution.py:23
  14.8 0.2 copy-done.1
  15.0 3.4 %fusion.22 = f32[512,8]{0,1:T(8,128)S(1)} fusion(f32[4096,8]{0,1:T(8,128)S(1)} %copy-done, bf16[512,4096]{1,0:T(8,128)(2,1)S(1)} %copy-done.1, f32[4096]{0:T(1024)S(1)} %copy-done.3, f32[512]{0:T(512)S(1)} %add_rsqrt_fusion), kind=kOutput, calls=%fused_computation.18 | convolution fusion | flops 209727488 | bytes 4360192 | tf_op jit(solution)/shard_map/dot_general | solution.py:26
  18.5 40.1 %all-gather.4.cloned.1.call-done = bf16[2,4096,256]{1,2,0:T(8,128)(2,1)} async-done(((bf16[2,512,256]{1,2,0:T(8,128)(2,1)}), bf16[2,4096,256]{1,2,0:T(8,128)(2,1)}) %all-gather.4.cloned.1.call-update) | async-done | bytes 4194320 | tf_op jit(solution)/shard_map/all_gather | solution.py:35
  58.6 5.9 %fusion.5 = f32[512,2,256]{0,2,1:T(8,128)S(1)} fusion(bf16[2,4096,256]{1,2,0:T(8,128)(2,1)} %all-gather.4.cloned.1.call-done, bf16[512,4096]{1,0:T(8,128)(2,1)} %param.7, f32[4096]{0:T(1024)S(1)} %copy-done.3, f32[512]{0:T(512)S(1)} %add_rsqrt_fusion), kind=kOutput, calls=%fused_computation.7 | convolution fusion | flops 2155872256 | bytes 9455616 | tf_op jit(solution)/shard_map/td,edf->tef/dot_general | solution.py:39
  64.5 41.4 %all-gather.6.cloned.1.call-done = bf16[2,4096,256]{1,2,0:T(8,128)(2,1)} async-done(((bf16[2,512,256]{1,2,0:T(8,128)(2,1)}), bf16[2,4096,256]{1,2,0:T(8,128)(2,1)}) %all-gather.6.cloned.1.call-update) | async-done | bytes 4194320 | tf_op jit(solution)/shard_map/all_gather | solution.py:36
  105.9 6.0 %fusion.17 = bf16[512,2,256]{0,2,1:T(8,128)(2,1)S(1)} fusion(bf16[2,4096,256]{1,2,0:T(8,128)(2,1)} %all-gather.6.cloned.1.call-done, f32[512,2,256]{0,2,1:T(8,128)S(1)} %fusion.5, f32[512,2]{0,1:T(2,128)S(1)} %fusion.24, bf16[512,4096]{1,0:T(8,128)(2,1)} %param.7, f32[4096]{0:T(1024)S(1)} %copy-done.3, f32[512]{0:T(512)S(1)} %add_rsqrt_fusion), kind=kOutput, calls=%fused_computation.14 | convolution fusion | flops 2157707264 | bytes 9984000 | tf_op jit(solution)/shard_map/td,edf->tef/dot_general | solution.py:40
  111.9 1.5 collective-permute-start
  113.4 13.5 %collective-permute-done = bf16[512,2,256]{0,2,1:T(8,128)(2,1)S(1)} collective-permute-done((bf16[512,2,256]{0,2,1:T(8,128)(2,1)S(1)}, bf16[512,2,256]{0,2,1:T(8,128)(2,1)S(1)}, u32[]{:S(2)}, u32[]{:S(2)}) %collective-permute-start) | collective-permute-done | bytes 524320 | tf_op jit(solution)/shard_map/ppermute | solution.py:15
  126.9 0.6 collective-permute-start.1
  127.5 13.6 %collective-permute-done.1 = bf16[512,2,256]{0,2,1:T(8,128)(2,1)S(1)} collective-permute-done((bf16[512,2,256]{0,2,1:T(8,128)(2,1)S(1)}, bf16[512,2,256]{0,2,1:T(8,128)(2,1)S(1)}, u32[]{:S(2)}, u32[]{:S(2)}) %collective-permute-start.1) | collective-permute-done | bytes 524320 | tf_op jit(solution)/shard_map/ppermute | solution.py:15
  141.1 13.4 %collective-permute-done.2 = bf16[512,2,256]{0,2,1:T(8,128)(2,1)S(1)} collective-permute-done((bf16[512,2,256]{0,2,1:T(8,128)(2,1)S(1)}, bf16[512,2,256]{0,2,1:T(8,128)(2,1)S(1)}, u32[]{:S(2)}, u32[]{:S(2)}) %collective-permute-start.2) | collective-permute-done | bytes 524320 | tf_op jit(solution)/shard_map/ppermute | solution.py:15
  154.6 0.8 constant_dynamic-update-slice_fusion.7
  155.4 0.8 constant_dynamic-update-slice_fusion.6
  156.2 0.8 constant_dynamic-update-slice_fusion.5
  157.1 0.9 constant_dynamic-update-slice_fusion.4
  157.9 0.8 constant_dynamic-update-slice_fusion.3
  158.8 0.8 constant_dynamic-update-slice_fusion.2
  159.6 0.8 constant_dynamic-update-slice_fusion.1
  160.4 0.9 constant_dynamic-update-slice_fusion
  161.3 6.1 %bitcast_convert_fusion = bf16[512,1024]{1,0:T(8,128)(2,1)} fusion(bf16[2,1024,1024]{2,1,0:T(8,128)(2,1)} %all-gather.8.cloned.1.call-done, bf16[512,2,2048]{0,2,1:T(8,128)(2,1)} %constant_dynamic-update-slice_fusion, s32[]{:T(128)S(6)} %select_n.14), kind=kOutput, calls=%fused_computation.9 | convolution fusion | flops 2148007936 | bytes 7340036 | tf_op jit(solution)/shard_map/tef,efd->td/dot_general | solution.py:43
  (17 shorter events, 0.2 us)
Async XLA Ops:
  6.5 8.3 %copy-start = (f32[4096,8]{0,1:T(8,128)S(1)}, f32[4096,8]{0,1:T(8,128)}, u32[]{:S(2)}) copy-start(f32[4096,8]{0,1:T(8,128)} %param.9) | copy-start | bytes 393220
  6.5 8.3 %copy-start.3 = (f32[4096]{0:T(1024)S(1)}, f32[4096]{0:T(1024)}, u32[]{:S(2)}) copy-start(f32[4096]{0:T(1024)} %param.8) | copy-start | bytes 49156
  6.5 52.0 %all-gather.4.cloned.1.call-start = ((), (), s32[]{:S(2)}) async-start(), calls=%async_computation | async-start | bytes 4718592 | tf_op jit(solution)/shard_map/all_gather | solution.py:35
  8.7 97.2 %all-gather.6.cloned.1.call-start = ((), (), s32[]{:S(2)}) async-start(), calls=%async_computation.1 | async-start | bytes 4718592 | tf_op jit(solution)/shard_map/all_gather | solution.py:36
  10.8 150.5 %all-gather.8.cloned.1.call-start = ((), (), s32[]{:S(2)}) async-start(), calls=%async_computation.2 | async-start | bytes 4718592 | tf_op jit(solution)/shard_map/all_gather | solution.py:37
  11.5 3.5 %copy-start.1 = (bf16[512,4096]{1,0:T(8,128)(2,1)S(1)}, bf16[512,4096]{1,0:T(8,128)(2,1)}, u32[]{:S(2)}) copy-start(bf16[512,4096]{1,0:T(8,128)(2,1)} %param.7) | copy-start | bytes 12582916
  14.8 3.6 %copy-start.2 = (s32[512,2]{0,1:T(2,128)S(1)}, s32[512,2]{0,1:T(2,128)}, u32[]{:S(2)}) copy-start(s32[512,2]{0,1:T(2,128)} %param.10) | copy-start | bytes 12292
  111.9 15.0 %collective-permute-start = (bf16[512,2,256]{0,2,1:T(8,128)(2,1)S(1)}, bf16[512,2,256]{0,2,1:T(8,128)(2,1)S(1)}, u32[]{:S(2)}, u32[]{:S(2)}) collective-permute-start(bf16[512,2,256]{0,2,1:T(8,128)(2,1)S(1)} %fusion.17), channel_id=1, source_target_pairs={{0,1},{1,2},{2,3},{3,0},{4,5},{5,6},{6,7},{7,4},{8,9},{9,10},{10,1... | collective-permute-start | bytes 1572872 | tf_op jit(solution)/shard_map/ppermute | solution.py:15
  126.9 14.2 %collective-permute-start.1 = (bf16[512,2,256]{0,2,1:T(8,128)(2,1)S(1)}, bf16[512,2,256]{0,2,1:T(8,128)(2,1)S(1)}, u32[]{:S(2)}, u32[]{:S(2)}) collective-permute-start(bf16[512,2,256]{0,2,1:T(8,128)(2,1)S(1)} %collective-permute-done), channel_id=1, source_target_pairs={{0,1},{1,2},{2,3},{3,0},{4,5},{5,6},{6,7},{7,4},{8,9},{9,10},{10,1... | collective-permute-start | bytes 1572872 | tf_op jit(solution)/shard_map/ppermute | solution.py:15
  141.1 13.5 %collective-permute-start.2 = (bf16[512,2,256]{0,2,1:T(8,128)(2,1)S(1)}, bf16[512,2,256]{0,2,1:T(8,128)(2,1)S(1)}, u32[]{:S(2)}, u32[]{:S(2)}) collective-permute-start(bf16[512,2,256]{0,2,1:T(8,128)(2,1)S(1)} %collective-permute-done.1), channel_id=1, source_target_pairs={{0,1},{1,2},{2,3},{3,0},{4,5},{5,6},{6,7},{7,4},{8,9},{9,10},{10,1... | collective-permute-start | bytes 1572872 | tf_op jit(solution)/shard_map/ppermute | solution.py:15
Sparse Core Ops, SparseCore 0:
  8.9 49.5 all-gather.3
  60.2 45.6 all-gather.5
  107.5 45.6 all-gather.7
